TPU v7x, 64 devices: a 2x2x8 block of a 4x4x8 slice. The times are simulated.
64 devices in a mesh: rep: 8 (over x, y, core), dp: 8 (over z).
Axes of the slice: x: 2, y: 2, z: 8, core: 2. Of those that a mesh axis runs over, the one named last changes fastest.
The devices are a block of a 4x4x8 slice.
Arguments:
- g_w_gate: bfloat16 [64, 2, 512, 1280], P(('rep', 'dp')), parts along dimension 0
- g_w_up: bfloat16 [64, 2, 512, 1280], P(('rep', 'dp')), parts along dimension 0
- g_w_down: bfloat16 [64, 2, 1280, 512], P(('rep', 'dp')), parts along dimension 0
- w_gate: bfloat16 [2, 512, 1280], replicated
- w_up: bfloat16 [2, 512, 1280], replicated
- w_down: bfloat16 [2, 1280, 512], replicated
- m_w_gate: float32 [2, 512, 1280], P(None, 'dp')
- m_w_up: float32 [2, 512, 1280], P(None, 'dp')
- m_w_down: float32 [2, 1280, 512], P(None, 'dp')
- v_w_gate: float32 [2, 512, 1280], P(None, 'dp')
- v_w_up: float32 [2, 512, 1280], P(None, 'dp')
- v_w_down: float32 [2, 1280, 512], P(None, 'dp')
Outputs:
- output 1: bfloat16 [16, 512, 1280], P('rep'), parts along dimension 0
- output 2: bfloat16 [16, 512, 1280], P('rep'), parts along dimension 0
- output 3: bfloat16 [16, 1280, 512], P('rep'), parts along dimension 0
- output 4: float32 [16, 512, 1280], P('rep', 'dp'), parts along dimension 0
- output 5: float32 [16, 512, 1280], P('rep', 'dp'), parts along dimension 0
- output 6: float32 [16, 1280, 512], P('rep', 'dp'), parts along dimension 0
- output 7: float32 [16, 512, 1280], P('rep', 'dp'), parts along dimension 0
- output 8: float32 [16, 512, 1280], P('rep', 'dp'), parts along dimension 0
- output 9: float32 [16, 1280, 512], P('rep', 'dp'), parts along dimension 0
There are 8 independent parts. A program takes and returns all parts, laid end to end along the dimension named above; an argument that names none is the same for every part.
All inputs are finite; a program needn't handle non-finite values.
Results may differ from a plain program's by a relative error of at most 0.022.
Values are sent between devices in bfloat16 or wider.
A program may use at most 768 MiB of HBM per device.

v0:
```python
import jax
import jax.numpy as jnp
from jax import lax
from jax.sharding import PartitionSpec as P


def adamw(w, m, v, g):
    m = 0.9 * m + 0.1 * g
    v = 0.95 * v + 0.05 * g * g
    step = m * lax.rsqrt(v + 1e-8) + 0.1 * w
    return (w - 0.02 * step).astype(jnp.bfloat16), m, v


def clipped(gradients, sum_of_squares, count):
    factor = jnp.minimum(1.0, 0.5 * lax.rsqrt(sum_of_squares / count + 1e-30))
    return [g * factor for g in gradients]


def solution(mesh):
    def step(*arrays):
        terms, weights, m, v = (arrays[i : i + 3] for i in (0, 3, 6, 9))
        gradients = [lax.psum_scatter(t[0], "dp", scatter_dimension=1, tiled=True).astype(jnp.float32) for t in terms]
        squares = lax.psum(sum(jnp.sum(g * g) for g in gradients), "dp")
        gradients = clipped(gradients, squares, lax.psum(1, "dp") * sum(g.size for g in gradients))
        me = lax.axis_index("dp")
        own = [lax.dynamic_slice_in_dim(w, me * one.shape[1], one.shape[1], 1).astype(jnp.float32) for w, one in zip(weights, m, strict=True)]
        new = [adamw(w, m, v, g) for w, m, v, g in zip(own, m, v, gradients, strict=True)]
        whole = [lax.all_gather(one[0], "dp", axis=1, tiled=True) for one in new]
        return (*whole, *(one[1] for one in new), *(one[2] for one in new))

    all_of, cut = P(None, None, None), P(None, "dp", None)
    return jax.shard_map(
        step,
        mesh=mesh,
        in_specs=(P(("rep", "dp"), None, None, None),) * 3 + (all_of,) * 3 + (cut,) * 6,
        out_specs=(P("rep", None, None),) * 3 + (P("rep", "dp", None),) * 6,
        check_vma=False,
    )
```

profile of v0, /device:TPU:22, one launch (start us, length us, event | category | flops | bytes accessed | tf_op | source)
XLA Modules:
  0.0 295.0 jit_solution(12033539479982468757)
XLA Ops:
  7.2 0.1 reduce-scatter.4.cloned.1.call-start
  7.3 0.7 reduce-scatter.4.cloned.1.call-update
  8.0 0.1 reduce-scatter.6.cloned.1.call-start
  8.1 0.0 copy-start.4
  8.1 0.0 copy-start.5
  8.1 0.7 reduce-scatter.6.cloned.1.call-update
  8.8 0.1 reduce-scatter.8.cloned.1.call-start
  8.9 0.7 reduce-scatter.8.cloned.1.call-update
  9.6 0.0 copy-start.6
  9.6 0.0 copy-start.7
  9.6 0.1 all-gather.8.cloned.1.call-start
  9.7 45.5 %reduce-scatter.4.cloned.1.call-done = bf16[2,64,1280]{2,1,0:T(8,128)(2,1)} async-done(((bf16[2,512,1280]{2,1,0:T(8,128)(2,1)}), bf16[2,64,1280]{2,1,0:T(8,128)(2,1)}) %reduce-scatter.4.cloned.1.call-update) | async-done | bytes 327696 | tf_op jit(solution)/shard_map/reduce_scatter | solution.py:22
  55.2 0.0 copy-start.3
  55.2 1.8 fusion.9
  57.0 40.8 %reduce-scatter.6.cloned.1.call-done = bf16[2,64,1280]{2,1,0:T(8,128)(2,1)} async-done(((bf16[2,512,1280]{2,1,0:T(8,128)(2,1)}), bf16[2,64,1280]{2,1,0:T(8,128)(2,1)}) %reduce-scatter.6.cloned.1.call-update) | async-done | bytes 327696 | tf_op jit(solution)/shard_map/reduce_scatter | solution.py:22
  97.8 1.7 fusion.10
  100.9 39.6 %reduce-scatter.8.cloned.1.call-done = bf16[2,160,512]{2,1,0:T(8,128)(2,1)} async-done(((bf16[2,1280,512]{2,1,0:T(8,128)(2,1)}), bf16[2,160,512]{2,1,0:T(8,128)(2,1)}) %reduce-scatter.8.cloned.1.call-update) | async-done | bytes 327696 | tf_op jit(solution)/shard_map/reduce_scatter | solution.py:22
  140.5 1.7 fusion.11
  142.9 16.1 %psum.7 = f32[]{:T(128)} all-reduce(f32[]{:T(128)S(6)} %add.65), channel_id=1, replica_groups=mesh['rep'=8,'dp'=8] {'dp'}, use_global_device_ids=true, to_apply=%region_6.0 | all-reduce | flops 1 | bytes 8 | tf_op jit(solution)/shard_map/psum | solution.py:23
  159.6 0.0 copy-done.4
  159.7 0.0 copy-done.5
  159.7 2.4 fusion.17
  162.1 0.0 copy-start.2
  162.1 0.0 copy-start.8
  162.1 0.1 all-gather.8.cloned.1.call-update
  162.2 0.1 all-gather.4.cloned.1.call-start
  162.2 0.0 copy-done.6
  162.3 0.0 copy-done.7
  162.3 0.0 copy-done.3
  162.3 2.4 fusion.8
  164.7 0.1 all-gather.4.cloned.1.call-update
  164.7 0.1 all-gather.6.cloned.1.call-start
  164.8 0.0 copy-done.2
  164.8 0.0 copy-done.8
  164.8 2.5 fusion.14
  167.4 0.1 all-gather.6.cloned.1.call-update
  167.4 33.6 %all-gather.8.cloned.1.call-done = bf16[2,1280,512]{2,1,0:T(8,128)(2,1)} async-done(((bf16[2,160,512]{2,1,0:T(8,128)(2,1)}), bf16[2,1280,512]{2,1,0:T(8,128)(2,1)}) %all-gather.8.cloned.1.call-update) | async-done | bytes 2621456 | tf_op jit(solution)/shard_map/all_gather | solution.py:28
  201.0 39.7 %all-gather.4.cloned.1.call-done = bf16[2,512,1280]{2,1,0:T(8,128)(2,1)} async-done(((bf16[2,64,1280]{2,1,0:T(8,128)(2,1)}), bf16[2,512,1280]{2,1,0:T(8,128)(2,1)}) %all-gather.4.cloned.1.call-update) | async-done | bytes 2621456 | tf_op jit(solution)/shard_map/all_gather | solution.py:28
  240.7 39.7 %all-gather.6.cloned.1.call-done = bf16[2,512,1280]{2,1,0:T(8,128)(2,1)} async-done(((bf16[2,64,1280]{2,1,0:T(8,128)(2,1)}), bf16[2,512,1280]{2,1,0:T(8,128)(2,1)}) %all-gather.6.cloned.1.call-update) | async-done | bytes 2621456 | tf_op jit(solution)/shard_map/all_gather | solution.py:28
  280.4 0.0 copy-start.1
  280.4 3.5 %copy.24 = bf16[2,512,1280]{2,1,0:T(8,128)(2,1)} copy(bf16[2,512,1280]{2,1,0:T(8,128)(2,1)} %all-gather.4.cloned.1.call-done) | data formatting | bytes 5242880
  283.9 0.0 copy-done.1
  283.9 0.0 copy-start
  283.9 1.5 copy.25
  285.4 1.2 copy-done
  286.6 1.5 copy.26
Async XLA Ops:
  7.2 48.0 %reduce-scatter.4.cloned.1.call-start = ((), (), s32[]{:S(2)}) async-start(), calls=%async_computation.3 | async-start | bytes 2949120 | tf_op jit(solution)/shard_map/reduce_scatter | solution.py:22
  8.0 89.9 %reduce-scatter.6.cloned.1.call-start = ((), (), s32[]{:S(2)}) async-start(), calls=%async_computation.4 | async-start | bytes 2949120 | tf_op jit(solution)/shard_map/reduce_scatter | solution.py:22
  8.1 151.6 %copy-start.4 = (f32[2,160,512]{2,1,0:T(8,128)S(1)}, f32[2,160,512]{2,1,0:T(8,128)}, u32[]{:S(2)}) copy-start(f32[2,160,512]{2,1,0:T(8,128)} %param.23) | copy-start | bytes 1966084
  8.1 151.6 %copy-start.5 = (f32[2,160,512]{2,1,0:T(8,128)S(1)}, f32[2,160,512]{2,1,0:T(8,128)}, u32[]{:S(2)}) copy-start(f32[2,160,512]{2,1,0:T(8,128)} %param.20) | copy-start | bytes 1966084
  8.8 131.7 %reduce-scatter.8.cloned.1.call-start = ((), (), s32[]{:S(2)}) async-start(), calls=%async_computation.5 | async-start | bytes 2949120 | tf_op jit(solution)/shard_map/reduce_scatter | solution.py:22
  9.6 152.7 %copy-start.6 = (f32[2,64,1280]{2,1,0:T(8,128)S(1)}, f32[2,64,1280]{2,1,0:T(8,128)}, u32[]{:S(2)}) copy-start(f32[2,64,1280]{2,1,0:T(8,128)} %param.21) | copy-start | bytes 1966084
  9.6 152.7 %copy-start.7 = (f32[2,64,1280]{2,1,0:T(8,128)S(1)}, f32[2,64,1280]{2,1,0:T(8,128)}, u32[]{:S(2)}) copy-start(f32[2,64,1280]{2,1,0:T(8,128)} %param.18) | copy-start | bytes 1966084
  9.6 191.4 %all-gather.8.cloned.1.call-start = ((), (), s32[]{:S(2)}) async-start(), calls=%async_computation.8 | async-start | bytes 2949120 | tf_op jit(solution)/shard_map/all_gather | solution.py:28
  55.2 107.0 %copy-start.3 = (bf16[2,64,1280]{2,1,0:T(8,128)(2,1)S(1)}, bf16[2,64,1280]{2,1,0:T(8,128)(2,1)}, u32[]{:S(2)}) copy-start(bf16[2,64,1280]{2,1,0:T(8,128)(2,1)} %reduce-scatter.4.cloned.1.call-done) | copy-start | bytes 983044
  162.1 2.7 copy-start.2
  162.1 2.7 copy-start.8
  162.2 78.5 %all-gather.4.cloned.1.call-start = ((), (), s32[]{:S(2)}) async-start(), calls=%async_computation.6 | async-start | bytes 2949120 | tf_op jit(solution)/shard_map/all_gather | solution.py:28
  164.7 115.7 %all-gather.6.cloned.1.call-start = ((), (), s32[]{:S(2)}) async-start(), calls=%async_computation.7 | async-start | bytes 2949120 | tf_op jit(solution)/shard_map/all_gather | solution.py:28
  280.4 3.6 %copy-start.1 = (bf16[2,512,1280]{2,1,0:T(8,128)(2,1)S(1)}, bf16[2,512,1280]{2,1,0:T(8,128)(2,1)}, u32[]{:S(2)}) copy-start(bf16[2,512,1280]{2,1,0:T(8,128)(2,1)} %all-gather.6.cloned.1.call-done) | copy-start | bytes 7864324
  283.9 2.7 copy-start
Sparse Core Ops, SparseCore 0:
  10.4 44.8 reduce-scatter.3
  57.6 40.2 reduce-scatter.5
  100.2 40.2 reduce-scatter.7
  162.3 38.6 all-gather.7
  203.0 37.6 all-gather.3
  242.7 37.6 all-gather.5
where the time goes:
time: 295 us
  waiting for transfers between devices  241 us (82%)
  between operations  16.9 us (6%)
  blocking collectives  16.1 us (5%)
  other arithmetic  12.7 us (4%)
  local copies, waits for them, and re-layouts  7.76 us (3%)
    reduce_scatter x3, waiting for transfers between devices, step(): lax.psum_scatter(t[0], 'dp', scatter_dimension=1, tiled=True)  126 us
    all_gather x3, waiting for transfers between devices, step(): whole = [lax.all_gather(one[0], 'dp', axis=1, tiled=True) for one in new]  113 us
    psum x1, blocking collectives, step(): squares = lax.psum(sum((jnp.sum(g * g) for g in gradients)), 'dp')  16.1 us
    unnamed x21, local copies, waits for them, and re-layouts  7.76 us
    convert_element_type x3, other arithmetic, adamw(): return ((w - 0.02 * step).astype(jnp.bfloat16), m, v)  7.36 us
  transfers between devices with their start and end apart: 6, of which 6 were waited for; matrix products, arithmetic and copies ran while one was open for 3% of the time, Pallas kernels for 0%

commit v1 on v0

v1 whole, which is shorter than its diff:
```python
import functools

import jax
import jax.numpy as jnp
from jax import lax
from jax.experimental import pallas as pl
from jax.experimental.pallas import tpu as pltpu
from jax.sharding import PartitionSpec as P

MESH = pl.DeviceIdType.MESH
F32, BF16 = jnp.float32, jnp.bfloat16
ROWS, LANES = 16, 256


def kernel(n, *refs):
    terms, weights, m_in, v_in = (refs[i : i + 3] for i in (0, 3, 6, 9))
    w_out, m_out, v_out = (refs[i : i + 3] for i in (12, 15, 18))
    own, arrived, total, w_old, w_new, m, v = (refs[i : i + 3] for i in (21, 24, 27, 30, 33, 36, 39))
    squares, load_sem, state_sem, out_sem, rs_send, rs_recv, sq_send, sq_recv, ag_send, ag_recv = refs[42:]

    half = n // 2
    me = lax.axis_index("dp")
    rows = [ref.shape[1] for ref in m_in]
    cols = [ref.shape[2] for ref in m_in]
    count = n * sum(2 * r * c for r, c in zip(rows, cols, strict=True))

    def at(offset):
        return lax.rem(me + offset + n, n)

    def block(weight, offset):
        return pl.multiple_of(at(offset) * rows[weight], rows[weight])

    def load(weight, offset):
        part = pl.ds(block(weight, offset), rows[weight])
        return pltpu.make_async_copy(terms[weight].at[:, part], own[weight].at[:, part], load_sem.at[weight, offset % n])

    order = [half]
    for distance in range(half - 1, 0, -1):
        order += [distance, -distance]
    order += [0]
    for offset in order:
        for weight in range(3):
            load(weight, offset).start()

    def state(which, weight):
        if which == 0:
            return pltpu.make_async_copy(weights[weight].at[:, pl.ds(block(weight, 0), rows[weight])], w_old[weight], state_sem.at[0, weight])
        source, target = ((m_in, m), (v_in, v))[which - 1]
        return pltpu.make_async_copy(source[weight], target[weight], state_sem.at[which, weight])

    for which in range(3):
        for weight in range(3):
            state(which, weight).start()

    barrier = pltpu.get_barrier_semaphore()
    for offset in (1, -1):
        pl.semaphore_signal(barrier, inc=1, device_id={"dp": at(offset)}, device_id_type=MESH)
    pl.semaphore_wait(barrier, 2)

    sign = (1, -1)
    sends = n - 1

    def distance(k):
        return half - (k + 1) // 2

    def layer(way, k):
        return (way + k) % 2

    def send_sum(way, k, weight):
        if k < 2:
            source = own[weight].at[layer(way, k), pl.ds(block(weight, sign[way] * distance(k)), rows[weight])]
        else:
            source = arrived[weight].at[way, k - 2]
        return pltpu.make_async_remote_copy(
            src_ref=source,
            dst_ref=arrived[weight].at[way, k],
            send_sem=rs_send.at[way, k, weight],
            recv_sem=rs_recv.at[way, k, weight],
            device_id={"dp": at(sign[way])},
            device_id_type=MESH,
        )

    loaded = set()

    def need(weight, offset):
        if (weight, offset % n) not in loaded:
            loaded.add((weight, offset % n))
            load(weight, offset).wait()

    for k in range(2):
        for weight in range(3):
            for way in range(2):
                need(weight, sign[way] * distance(k))
                send_sum(way, k, weight).start()

    def pieces(weight, body, carry=None):
        def step(i, carry):
            r = pl.multiple_of(i * ROWS, ROWS)
            for c in range(0, cols[weight], LANES):
                carry = body(r, pl.ds(c, LANES), carry)
            return carry

        return lax.fori_loop(0, rows[weight] // ROWS, step, carry)

    def add(way, k, weight):
        offset, which = sign[way] * (distance(k) - 1), layer(way, k)
        base = block(weight, offset)

        def body(r, c, carry):
            term = own[weight][which, pl.ds(pl.multiple_of(base + r, ROWS), ROWS), c].astype(F32)
            so_far = arrived[weight][way, k, pl.ds(r, ROWS), c].astype(F32)
            arrived[weight][way, k, pl.ds(r, ROWS), c] = (so_far + term).astype(BF16)
            return carry

        pieces(weight, body, 0)

    for k in range(sends - 2):
        for weight in range(3):
            for way in range(2):
                need(weight, sign[way] * (distance(k) - 1))
                send_sum(way, k, weight).wait_recv()
                add(way, k, weight)
                send_sum(way, k + 2, weight).start()

    def finish(which, weight, sums):
        base = block(weight, 0)
        first, second = ((way, k) for way in range(2) for k in (sends - 2, sends - 1) if layer(way, k) == which)

        def body(r, c, sums):
            g = own[weight][which, pl.ds(pl.multiple_of(base + r, ROWS), ROWS), c].astype(F32)
            g += arrived[weight][first[0], first[1], pl.ds(r, ROWS), c].astype(F32)
            g += arrived[weight][second[0], second[1], pl.ds(r, ROWS), c].astype(F32)
            g = g.astype(BF16)
            total[weight][which, pl.ds(r, ROWS), c] = g
            g = g.astype(F32)
            g = g * g
            return sums + (g[:8] + g[8:])

        return pieces(weight, body, sums)

    for weight in range(3):
        need(weight, 0)
        for way in range(2):
            send_sum(way, sends - 2, weight).wait_recv()
    sums = jnp.zeros((8, LANES), F32)
    for weight in range(3):
        for way in range(2):
            send_sum(way, sends - 1, weight).wait_recv()
            sums = finish(layer(way, sends - 1), weight, sums)
    sums = sum(sums[:, c : c + 128] for c in range(0, LANES, 128))
    squares[0] = jnp.broadcast_to(jnp.sum(sums, axis=0, keepdims=True), (8, 128))

    def send_squares(offset):
        return pltpu.make_async_remote_copy(
            src_ref=squares.at[0],
            dst_ref=squares.at[offset],
            send_sem=sq_send.at[offset],
            recv_sem=sq_recv.at[offset],
            device_id={"dp": at(offset)},
            device_id_type=MESH,
        )

    far_first = sorted(range(1, n), key=lambda offset: -min(offset, n - offset))
    for offset in far_first:
        send_squares(offset).start()
    for which in range(3):
        for weight in range(3):
            state(which, weight).wait()
    everyone = squares[0, :1]
    for offset in reversed(far_first):
        send_squares(offset).wait_recv()
        everyone += squares[offset, :1]
    everyone = jnp.sum(everyone, axis=1, keepdims=True)
    factor = jnp.minimum(1.0, 0.5 * lax.rsqrt(everyone / count + 1e-30))

    def adamw(which, weight):
        def body(r, c, carry):
            part = (which, pl.ds(r, ROWS), c)
            g = total[weight][part].astype(F32) * factor
            w = w_old[weight][part].astype(F32)
            m_new = 0.9 * m[weight][part] + 0.1 * g
            v_new = 0.95 * v[weight][part] + 0.05 * g * g
            m[weight][part] = m_new
            v[weight][part] = v_new
            step = m_new * lax.rsqrt(v_new + 1e-8) + 0.1 * w
            w_new[weight][part] = (w - 0.02 * step).astype(BF16)
            return carry

        pieces(weight, body, 0)

    def send_new(way, q, which, weight):
        part = pl.ds(block(weight, -sign[way] * q), rows[weight])
        place = w_out[weight].at[which, part]
        return pltpu.make_async_remote_copy(
            src_ref=w_new[weight].at[which] if q == 0 else place,
            dst_ref=place,
            send_sem=ag_send.at[way, q, which, weight],
            recv_sem=ag_recv.at[way, q, which, weight],
            device_id={"dp": at(sign[way])},
            device_id_type=MESH,
        )

    def recv_new(way, q, which, weight):
        part = pl.ds(block(weight, -sign[way] * (q + 1)), rows[weight])
        place = w_out[weight].at[which, part]
        return pltpu.make_async_remote_copy(
            src_ref=place,
            dst_ref=place,
            send_sem=ag_send.at[way, q, which, weight],
            recv_sem=ag_recv.at[way, q, which, weight],
            device_id={"dp": at(sign[way])},
            device_id_type=MESH,
        )

    def keep(which, weight, what):
        if what == 0:
            part = pl.ds(block(weight, 0), rows[weight])
            return pltpu.make_async_copy(w_new[weight].at[which], w_out[weight].at[which, part], out_sem.at[0, which, weight])
        source, target = ((m, m_out), (v, v_out))[what - 1]
        return pltpu.make_async_copy(source[weight].at[which], target[weight].at[which], out_sem.at[what, which, weight])

    for which in range(2):
        for weight in range(3):
            adamw(which, weight)
            for way in range(2):
                send_new(way, 0, which, weight).start()
            for what in range(3):
                keep(which, weight, what).start()
    for q in range(half):
        for which in range(2):
            for weight in range(3):
                for way in range(2):
                    if q == half - 1 and which != way:
                        continue
                    recv_new(way, q, which, weight).wait_recv()
                    if q + 1 < half - 1 or (q + 1 == half - 1 and which == way):
                        send_new(way, q + 1, which, weight).start()

    for weight in range(3):
        for way in range(2):
            for k in range(sends):
                send_sum(way, k, weight).wait_send()
            for q in range(half):
                for which in range(2):
                    if q < half - 1 or which == way:
                        send_new(way, q, which, weight).wait_send()
        for which in range(2):
            for what in range(3):
                keep(which, weight, what).wait()
    for offset in far_first:
        send_squares(offset).wait_send()


def solution(mesh):
    n = mesh.shape["dp"]

    def step(*arrays):
        terms, weights, m, v = (arrays[i : i + 3] for i in (0, 3, 6, 9))
        terms = tuple(t[0] for t in terms)
        half = n // 2
        shapes = [one.shape for one in m]
        dma = pltpu.SemaphoreType.DMA
        out = [jax.ShapeDtypeStruct(w.shape, w.dtype) for w in weights]
        out += [jax.ShapeDtypeStruct(one.shape, one.dtype) for one in (*m, *v)]
        scratch = [pltpu.VMEM(t.shape, t.dtype) for t in terms]
        scratch += [pltpu.VMEM((2, n - 1, *s[1:]), BF16) for s in shapes]
        scratch += [pltpu.VMEM(s, BF16) for _ in range(3) for s in shapes]
        scratch += [pltpu.VMEM(s, F32) for _ in range(2) for s in shapes]
        scratch += [
            pltpu.VMEM((n, 8, 128), F32),
            dma((3, n)),
            dma((3, 3)),
            dma((3, 2, 3)),
            dma((2, n - 1, 3)),
            dma((2, n - 1, 3)),
            dma((n,)),
            dma((n,)),
            dma((2, half, 2, 3)),
            dma((2, half, 2, 3)),
        ]
        return pl.pallas_call(
            functools.partial(kernel, n),
            out_shape=out,
            in_specs=[pl.BlockSpec(memory_space=pltpu.HBM)] * 12,
            out_specs=[pl.BlockSpec(memory_space=pl.ANY)] * 9,
            scratch_shapes=scratch,
            compiler_params=pltpu.CompilerParams(collective_id=0, has_side_effects=True, vmem_limit_bytes=40 * 2**20),
        )(*terms, *weights, *m, *v)

    all_of, cut = P(None, None, None), P(None, "dp", None)
    return jax.shard_map(
        step,
        mesh=mesh,
        in_specs=(P(("rep", "dp"), None, None, None),) * 3 + (all_of,) * 3 + (cut,) * 6,
        out_specs=(P("rep", None, None),) * 3 + (P("rep", "dp", None),) * 6,
        check_vma=False,
    )
```

time: 295 us -> 184 us (0.62)
  waiting for transfers between devices: 241 us -> 0 us
  Pallas kernels: 0 us -> 165 us
  between operations: 16.9 us -> 0.67 us
  blocking collectives: 16.1 us -> 0 us
  other arithmetic: 12.7 us -> 0 us
  local copies, waits for them, and re-layouts: 7.76 us -> 17.2 us
    pallas_call x0 -> x1, Pallas kernels: none -> 165 us  [step(): pl.pallas_call(functools.partial(kernel, n), out_shape=out, in_specs=[pl....]
    reduce_scatter x3 -> x0, waiting for transfers between devices: 126 us -> none  [step(): lax.psum_scatter(t[0], 'dp', scatter_dimension=1, tiled=True)]
    all_gather x3 -> x0, waiting for transfers between devices: 113 us -> none  [step(): whole = [lax.all_gather(one[0], 'dp', axis=1, tiled=True) for one in new]]
    psum x1 -> x0, blocking collectives: 16.1 us -> none  [step(): squares = lax.psum(sum((jnp.sum(g * g) for g in gradients)), 'dp')]
    unnamed x21 -> x23, local copies, waits for them, and re-layouts: 7.76 us -> 17.2 us
    convert_element_type x3 -> x0, other arithmetic: 7.36 us -> none  [adamw(): return ((w - 0.02 * step).astype(jnp.bfloat16), m, v)]
    reduce_sum x3 -> x0, other arithmetic: 5.31 us -> none  [step(): squares = lax.psum(sum((jnp.sum(g * g) for g in gradients)), 'dp')]
  transfers between devices with their start and end apart: 6 -> 0, of which waited for: 6 -> 0; matrix products, arithmetic and copies ran while one was open for 3% -> 0% of each run, Pallas kernels for 0% -> 0%
where the time goes in v1:
time: 184 us; the launch traced here: 183 us
  Pallas kernels  165 us (90%)
  local copies, waits for them, and re-layouts  17.2 us (9%)
    pallas_call x1, Pallas kernels, step(): pl.pallas_call(functools.partial(kernel, n), out_shape=out, in_specs=[pl....  165 us
    unnamed x23, local copies, waits for them, and re-layouts  17.2 us

profile of v1, /device:TPU:22, one launch (start us, length us, event | category | flops | bytes accessed | tf_op | source)
XLA Modules:
  0.0 183.2 jit_solution(8223932609345218779)
XLA Ops:
  0.6 0.0 copy-start
  0.7 1.1 copy-done
  1.7 0.0 copy-start.1
  1.7 1.1 copy-done.1
  2.8 0.0 copy-start.2
  2.8 1.1 copy-done.2
  3.9 0.0 copy-start.3
  3.9 1.1 copy-done.3
  5.0 0.0 copy-start.4
  5.0 1.1 copy-done.4
  6.1 0.0 copy-start.5
  6.1 1.1 copy-done.5
  7.2 165.3 %shard_map.187 = (bf16[2,512,1280]{2,1,0:T(8,128)(2,1)S(1)}, bf16[2,512,1280]{2,1,0:T(8,128)(2,1)S(1)}, bf16[2,1280,512]{2,1,0:T(8,128)(2,1)}, f32[2,64,1280]{2,...) custom-call(bf16[2,512,1280]{2,1,0:T(8,128)(2,1)} %bitcast.3, ...), custom_call_target="tpu_custom_call" | custom-call | tf_op jit(solution)/shard_map/pallas_call | solution.py:281
  172.5 1.5 copy.30
  174.0 0.0 copy-start.6
  174.0 1.5 copy.31
  175.5 1.2 copy-done.6
  176.7 1.5 copy.32
  178.2 0.8 copy.33
  179.0 0.8 copy.34
  179.9 0.8 copy.35
  180.7 0.8 copy.36
  181.5 0.8 copy.37
  182.4 0.8 copy.38
Async XLA Ops:
  0.6 1.1 copy-start
  1.7 1.1 copy-start.1
  2.8 1.1 copy-start.2
  3.9 1.1 copy-start.3
  5.0 1.1 copy-start.4
  6.1 1.1 copy-start.5
  174.0 2.7 %copy-start.6 = (bf16[2,1280,512]{2,1,0:T(8,128)(2,1)S(1)}, bf16[2,1280,512]{2,1,0:T(8,128)(2,1)}, u32[]{:S(2)}) copy-start(bf16[2,1280,512]{2,1,0:T(8,128)(2,1)} %get-tuple-element.20) | copy-start | bytes 7864324

commit v2 on v1

--- a/solution.py
+++ b/solution.py
@@ -15,8 +15,8 @@
 def kernel(n, *refs):
     terms, weights, m_in, v_in = (refs[i : i + 3] for i in (0, 3, 6, 9))
     w_out, m_out, v_out = (refs[i : i + 3] for i in (12, 15, 18))
-    own, arrived, total, w_old, w_new, m, v = (refs[i : i + 3] for i in (21, 24, 27, 30, 33, 36, 39))
-    squares, load_sem, state_sem, out_sem, rs_send, rs_recv, sq_send, sq_recv, ag_send, ag_recv = refs[42:]
+    own, arrived, total, w_old, m, v = (refs[i : i + 3] for i in (21, 24, 27, 30, 33, 36))
+    squares, load_sem, state_sem, rs_send, rs_recv, sq_send, sq_recv, ag_send, ag_recv = refs[39:]
 
     half = n // 2
     me = lax.axis_index("dp")
@@ -174,16 +174,18 @@
     factor = jnp.minimum(1.0, 0.5 * lax.rsqrt(everyone / count + 1e-30))
 
     def adamw(which, weight):
+        base = block(weight, 0)
+
         def body(r, c, carry):
             part = (which, pl.ds(r, ROWS), c)
             g = total[weight][part].astype(F32) * factor
             w = w_old[weight][part].astype(F32)
             m_new = 0.9 * m[weight][part] + 0.1 * g
             v_new = 0.95 * v[weight][part] + 0.05 * g * g
-            m[weight][part] = m_new
-            v[weight][part] = v_new
+            m_out[weight][part] = m_new
+            v_out[weight][part] = v_new
             step = m_new * lax.rsqrt(v_new + 1e-8) + 0.1 * w
-            w_new[weight][part] = (w - 0.02 * step).astype(BF16)
+            w_out[weight][which, pl.ds(pl.multiple_of(base + r, ROWS), ROWS), c] = (w - 0.02 * step).astype(BF16)
             return carry
 
         pieces(weight, body, 0)
@@ -192,7 +194,7 @@
         part = pl.ds(block(weight, -sign[way] * q), rows[weight])
         place = w_out[weight].at[which, part]
         return pltpu.make_async_remote_copy(
-            src_ref=w_new[weight].at[which] if q == 0 else place,
+            src_ref=place,
             dst_ref=place,
             send_sem=ag_send.at[way, q, which, weight],
             recv_sem=ag_recv.at[way, q, which, weight],
@@ -212,20 +214,11 @@
             device_id_type=MESH,
         )
 
-    def keep(which, weight, what):
-        if what == 0:
-            part = pl.ds(block(weight, 0), rows[weight])
-            return pltpu.make_async_copy(w_new[weight].at[which], w_out[weight].at[which, part], out_sem.at[0, which, weight])
-        source, target = ((m, m_out), (v, v_out))[what - 1]
-        return pltpu.make_async_copy(source[weight].at[which], target[weight].at[which], out_sem.at[what, which, weight])
-
     for which in range(2):
         for weight in range(3):
             adamw(which, weight)
             for way in range(2):
                 send_new(way, 0, which, weight).start()
-            for what in range(3):
-                keep(which, weight, what).start()
     for q in range(half):
         for which in range(2):
             for weight in range(3):
@@ -244,11 +237,18 @@
                 for which in range(2):
                     if q < half - 1 or which == way:
                         send_new(way, q, which, weight).wait_send()
-        for which in range(2):
-            for what in range(3):
-                keep(which, weight, what).wait()
     for offset in far_first:
         send_squares(offset).wait_send()
+
+
+def put_out(*refs):
+    arrays = len(refs) // 2
+    sem = refs[-1]
+    copies = [pltpu.make_async_copy(refs[i].at[half], refs[arrays + i].at[half], sem.at[i, half]) for i in range(arrays) for half in range(2)]
+    for copy in copies:
+        copy.start()
+    for copy in copies:
+        copy.wait()
 
 
 def solution(mesh):
@@ -264,13 +264,12 @@
         out += [jax.ShapeDtypeStruct(one.shape, one.dtype) for one in (*m, *v)]
         scratch = [pltpu.VMEM(t.shape, t.dtype) for t in terms]
         scratch += [pltpu.VMEM((2, n - 1, *s[1:]), BF16) for s in shapes]
-        scratch += [pltpu.VMEM(s, BF16) for _ in range(3) for s in shapes]
+        scratch += [pltpu.VMEM(s, BF16) for _ in range(2) for s in shapes]
         scratch += [pltpu.VMEM(s, F32) for _ in range(2) for s in shapes]
         scratch += [
             pltpu.VMEM((n, 8, 128), F32),
             dma((3, n)),
             dma((3, 3)),
-            dma((3, 2, 3)),
             dma((2, n - 1, 3)),
             dma((2, n - 1, 3)),
             dma((n,)),
@@ -278,14 +277,23 @@
             dma((2, half, 2, 3)),
             dma((2, half, 2, 3)),
         ]
+        in_hbm = [pltpu.with_memory_space_constraint(one, pltpu.HBM) for one in (*terms, *weights, *m, *v)]
+        new = pl.pallas_call(
+            functools.partial(kernel, n),
+            out_shape=[pltpu.VMEM(one.shape, one.dtype) for one in out],
+            in_specs=[pl.BlockSpec(memory_space=pltpu.HBM)] * len(in_hbm),
+            out_specs=[pl.BlockSpec(memory_space=pltpu.VMEM)] * len(out),
+            scratch_shapes=scratch,
+            compiler_params=pltpu.CompilerParams(collective_id=0, has_side_effects=True, vmem_limit_bytes=28 * 2**20),
+        )(*in_hbm)
         return pl.pallas_call(
-            functools.partial(kernel, n),
+            put_out,
             out_shape=out,
-            in_specs=[pl.BlockSpec(memory_space=pltpu.HBM)] * 12,
-            out_specs=[pl.BlockSpec(memory_space=pl.ANY)] * 9,
-            scratch_shapes=scratch,
-            compiler_params=pltpu.CompilerParams(collective_id=0, has_side_effects=True, vmem_limit_bytes=40 * 2**20),
-        )(*terms, *weights, *m, *v)
+            in_specs=[pl.BlockSpec(memory_space=pltpu.VMEM)] * len(out),
+            out_specs=[pl.BlockSpec(memory_space=pl.ANY)] * len(out),
+            scratch_shapes=[dma((len(out), 2))],
+            compiler_params=pltpu.CompilerParams(vmem_limit_bytes=2**20),
+        )(*(pltpu.with_memory_space_constraint(one, pltpu.VMEM) for one in new))
 
     all_of, cut = P(None, None, None), P(None, "dp", None)
     return jax.shard_map(

time: 184 us -> 169 us (0.918)
  local copies, waits for them, and re-layouts: 17.2 us -> 0 us
  Pallas kernels: 165 us -> 168 us
    unnamed x23 -> x0, local copies, waits for them, and re-layouts: 17.2 us -> none
    pallas_call x1 -> x2, Pallas kernels: 165 us -> 168 us  [the longest x1 164 us: step(): pl.pallas_call(functools.partial(kernel, n), out_shape=[pltpu.VMEM(one.sh...]
where the time goes in v2:
time: 169 us
  Pallas kernels  168 us (99%)
    pallas_call x1, Pallas kernels, step(): pl.pallas_call(functools.partial(kernel, n), out_shape=[pltpu.VMEM(one.sh...  164 us
    pallas_call x1, Pallas kernels, step(): pl.pallas_call(put_out, out_shape=out, in_specs=[pl.BlockSpec(memory_spac...  4.49 us

profile of v2, /device:TPU:22, one launch (start us, length us, event | category | flops | bytes accessed | tf_op | source)
XLA Modules:
  0.0 169.0 jit_solution(17608551670886622468)
XLA Ops:
  0.6 163.9 %shard_map.187 = (bf16[2,512,1280]{2,1,0:T(8,128)(2,1)S(1)}, bf16[2,512,1280]{2,1,0:T(8,128)(2,1)S(1)}, bf16[2,1280,512]{2,1,0:T(8,128)(2,1)S(1)}, f32[2,64,1280...) custom-call(bf16[2,512,1280]{2,1,0:T(8,128)(2,1)} %bitcast.3, ...), custom_call_target="tpu_custom_call" | custom-call | tf_op jit(solution)/shard_map/pallas_call | solution.py:281
  164.5 4.5 %shard_map.188 = (bf16[2,512,1280]{2,1,0:T(8,128)(2,1)}, bf16[2,512,1280]{2,1,0:T(8,128)(2,1)}, bf16[2,1280,512]{2,1,0:T(8,128)(2,1)}, f32[2,64,1280]{2,1,0:T(8,...) custom-call(bf16[2,512,1280]{2,1,0:T(8,128)(2,1)S(1)} %get-tuple-ele, ...), custom_call_target="tpu_custom_call" | custom-call | tf_op jit(solution)/shard_map/pallas_call | solution.py:289

commit v3 on v2

--- a/solution.py
+++ b/solution.py
@@ -11,12 +11,14 @@
 F32, BF16 = jnp.float32, jnp.bfloat16
 ROWS, LANES = 16, 256
 
-
-def kernel(n, *refs):
+LATE, HEAD_START_NS = 0, 13000
+
+
+def reduce_and_step(n, *refs):
     terms, weights, m_in, v_in = (refs[i : i + 3] for i in (0, 3, 6, 9))
     w_out, m_out, v_out = (refs[i : i + 3] for i in (12, 15, 18))
     own, arrived, total, w_old, m, v = (refs[i : i + 3] for i in (21, 24, 27, 30, 33, 36))
-    squares, load_sem, state_sem, rs_send, rs_recv, sq_send, sq_recv, ag_send, ag_recv = refs[39:]
+    squares, load_sem, state_sem, rs_send, rs_recv, sq_send, sq_recv = refs[39:]
 
     half = n // 2
     me = lax.axis_index("dp")
@@ -87,6 +89,10 @@
             loaded.add((weight, offset % n))
             load(weight, offset).wait()
 
+    @pl.when(lax.rem(lax.axis_index("rep"), 2) == LATE)
+    def _():
+        pl.delay(HEAD_START_NS)
+
     for k in range(2):
         for weight in range(3):
             for way in range(2):
@@ -121,6 +127,7 @@
                 send_sum(way, k, weight).wait_recv()
                 add(way, k, weight)
                 send_sum(way, k + 2, weight).start()
+                send_sum(way, k, weight).wait_send()
 
     def finish(which, weight, sums):
         base = block(weight, 0)
@@ -163,9 +170,12 @@
     far_first = sorted(range(1, n), key=lambda offset: -min(offset, n - offset))
     for offset in far_first:
         send_squares(offset).start()
-    for which in range(3):
-        for weight in range(3):
+    for weight in range(3):
+        for which in range(3):
             state(which, weight).wait()
+        for way in range(2):
+            for k in range(sends - 2, sends):
+                send_sum(way, k, weight).wait_send()
     everyone = squares[0, :1]
     for offset in reversed(far_first):
         send_squares(offset).wait_recv()
@@ -174,8 +184,6 @@
     factor = jnp.minimum(1.0, 0.5 * lax.rsqrt(everyone / count + 1e-30))
 
     def adamw(which, weight):
-        base = block(weight, 0)
-
         def body(r, c, carry):
             part = (which, pl.ds(r, ROWS), c)
             g = total[weight][part].astype(F32) * factor
@@ -185,66 +193,90 @@
             m_out[weight][part] = m_new
             v_out[weight][part] = v_new
             step = m_new * lax.rsqrt(v_new + 1e-8) + 0.1 * w
-            w_out[weight][which, pl.ds(pl.multiple_of(base + r, ROWS), ROWS), c] = (w - 0.02 * step).astype(BF16)
+            w_out[weight][part] = (w - 0.02 * step).astype(BF16)
             return carry
 
         pieces(weight, body, 0)
 
-    def send_new(way, q, which, weight):
-        part = pl.ds(block(weight, -sign[way] * q), rows[weight])
-        place = w_out[weight].at[which, part]
+    for which in range(2):
+        for weight in range(3):
+            adamw(which, weight)
+
+    for offset in far_first:
+        send_squares(offset).wait_send()
+
+
+def gather(n, count, *refs):
+    blocks, whole = refs[:count], refs[count + 1 : 2 * count + 1]
+    sends, recvs = refs[2 * count + 1 :]
+    half = n // 2
+    me = lax.axis_index("dp")
+    sign = (1, -1)
+
+    def at(offset):
+        return lax.rem(me + offset + n, n)
+
+    barrier = pltpu.get_barrier_semaphore()
+    for offset in sign:
+        pl.semaphore_signal(barrier, inc=1, device_id={"dp": at(offset)}, device_id_type=MESH)
+    pl.semaphore_wait(barrier, 2)
+
+    def copy(way, q, which, weight, behind):
+        rows = blocks[weight].shape[1]
+        place = whole[weight].at[which, pl.ds(pl.multiple_of(at(-sign[way] * behind) * rows, rows), rows)]
         return pltpu.make_async_remote_copy(
-            src_ref=place,
+            src_ref=blocks[weight].at[which] if behind == 0 else place,
             dst_ref=place,
-            send_sem=ag_send.at[way, q, which, weight],
-            recv_sem=ag_recv.at[way, q, which, weight],
+            send_sem=sends.at[way, q, which, weight],
+            recv_sem=recvs.at[way, q, which, weight],
             device_id={"dp": at(sign[way])},
             device_id_type=MESH,
         )
 
-    def recv_new(way, q, which, weight):
-        part = pl.ds(block(weight, -sign[way] * (q + 1)), rows[weight])
-        place = w_out[weight].at[which, part]
-        return pltpu.make_async_remote_copy(
-            src_ref=place,
-            dst_ref=place,
-            send_sem=ag_send.at[way, q, which, weight],
-            recv_sem=ag_recv.at[way, q, which, weight],
-            device_id={"dp": at(sign[way])},
-            device_id_type=MESH,
-        )
-
+    def goes(way, q, which):
+        return q < half - 1 or (q == half - 1 and which == way)
+
+    for q in range(half + 1):
+        for which in range(2):
+            for weight in range(count):
+                for way in range(2):
+                    if q and goes(way, q - 1, which):
+                        copy(way, q - 1, which, weight, q).wait_recv()
+                    if goes(way, q, which):
+                        copy(way, q, which, weight, q).start()
+                    if q > 1:
+                        copy(way, q - 2, which, weight, q - 2).wait_send()
     for which in range(2):
-        for weight in range(3):
-            adamw(which, weight)
-            for way in range(2):
-                send_new(way, 0, which, weight).start()
-    for q in range(half):
-        for which in range(2):
-            for weight in range(3):
-                for way in range(2):
-                    if q == half - 1 and which != way:
-                        continue
-                    recv_new(way, q, which, weight).wait_recv()
-                    if q + 1 < half - 1 or (q + 1 == half - 1 and which == way):
-                        send_new(way, q + 1, which, weight).start()
-
-    for weight in range(3):
-        for way in range(2):
-            for k in range(sends):
-                send_sum(way, k, weight).wait_send()
-            for q in range(half):
-                for which in range(2):
-                    if q < half - 1 or which == way:
-                        send_new(way, q, which, weight).wait_send()
-    for offset in far_first:
-        send_squares(offset).wait_send()
-
-
-def put_out(*refs):
-    arrays = len(refs) // 2
+        for weight in range(count):
+            copy(which, half - 1, which, weight, half - 1).wait_send()
+
+
+def put_state(*refs):
+    arrays = len(refs) // 2 - 1
     sem = refs[-1]
-    copies = [pltpu.make_async_copy(refs[i].at[half], refs[arrays + i].at[half], sem.at[i, half]) for i in range(arrays) for half in range(2)]
+    copies = [
+        pltpu.make_async_copy(refs[i].at[layer], refs[arrays + i].at[layer], sem.at[i, layer])
+        for i in range(arrays)
+        for layer in range(2)
+    ]
+    for copy in copies:
+        copy.start()
+    for copy in copies:
+        copy.wait()
+
+
+def put_weights(n, count, *refs):
+    blocks, whole, out = refs[:count], refs[count : 2 * count], refs[2 * count : 3 * count]
+    sem = refs[-1]
+    me = lax.axis_index("dp")
+    copies = []
+    for i in range(count):
+        rows = blocks[i].shape[1]
+        for layer in range(2):
+            for offset in range(n):
+                part = pl.ds(pl.multiple_of(lax.rem(me + offset, n) * rows, rows), rows)
+                source = blocks[i].at[layer] if offset == 0 else whole[i].at[layer, part]
+                copies.append(pltpu.make_async_copy(source, out[i].at[layer, part], sem.at[i, layer, offset]))
     for copy in copies:
         copy.start()
     for copy in copies:
@@ -260,8 +292,6 @@
         half = n // 2
         shapes = [one.shape for one in m]
         dma = pltpu.SemaphoreType.DMA
-        out = [jax.ShapeDtypeStruct(w.shape, w.dtype) for w in weights]
-        out += [jax.ShapeDtypeStruct(one.shape, one.dtype) for one in (*m, *v)]
         scratch = [pltpu.VMEM(t.shape, t.dtype) for t in terms]
         scratch += [pltpu.VMEM((2, n - 1, *s[1:]), BF16) for s in shapes]
         scratch += [pltpu.VMEM(s, BF16) for _ in range(2) for s in shapes]
@@ -274,26 +304,50 @@
             dma((2, n - 1, 3)),
             dma((n,)),
             dma((n,)),
-            dma((2, half, 2, 3)),
-            dma((2, half, 2, 3)),
         ]
+        hbm, vmem, anywhere = (pl.BlockSpec(memory_space=space) for space in (pltpu.HBM, pltpu.VMEM, pl.ANY))
+
+        def in_vmem(arrays):
+            return [pltpu.with_memory_space_constraint(one, pltpu.VMEM) for one in arrays]
+
+        def plain(body, arrays, out, sems):
+            token = jax.ShapeDtypeStruct((8, 128), F32)
+            *out, token = pl.pallas_call(
+                body,
+                out_shape=[*(jax.ShapeDtypeStruct(one.shape, one.dtype) for one in out), token],
+                in_specs=[vmem] * len(arrays),
+                out_specs=[anywhere] * (len(out) + 1),
+                scratch_shapes=[dma(sems)],
+                compiler_params=pltpu.CompilerParams(vmem_limit_bytes=2**20, has_side_effects=True),
+            )(*in_vmem(arrays))
+            return out, token
+
+        def gathered(blocks, shapes, token, collective_id):
+            count = len(blocks)
+            whole = pl.pallas_call(
+                functools.partial(gather, n, count),
+                out_shape=[pltpu.VMEM(one.shape, one.dtype) for one in shapes],
+                in_specs=[vmem] * count + [anywhere],
+                out_specs=[vmem] * count,
+                scratch_shapes=[dma((2, half, 2, count))] * 2,
+                compiler_params=pltpu.CompilerParams(collective_id=collective_id, has_side_effects=True, vmem_limit_bytes=2**20),
+            )(*in_vmem(blocks), token)
+            return plain(functools.partial(put_weights, n, count), (*blocks, *whole), shapes, (count, 2, n))
+
         in_hbm = [pltpu.with_memory_space_constraint(one, pltpu.HBM) for one in (*terms, *weights, *m, *v)]
+        results = [(s, BF16) for s in shapes] + [(s, F32) for s in shapes] * 2
         new = pl.pallas_call(
-            functools.partial(kernel, n),
-            out_shape=[pltpu.VMEM(one.shape, one.dtype) for one in out],
-            in_specs=[pl.BlockSpec(memory_space=pltpu.HBM)] * len(in_hbm),
-            out_specs=[pl.BlockSpec(memory_space=pltpu.VMEM)] * len(out),
+            functools.partial(reduce_and_step, n),
+            out_shape=[pltpu.VMEM(*one) for one in results],
+            in_specs=[hbm] * len(in_hbm),
+            out_specs=[vmem] * len(results),
             scratch_shapes=scratch,
             compiler_params=pltpu.CompilerParams(collective_id=0, has_side_effects=True, vmem_limit_bytes=28 * 2**20),
         )(*in_hbm)
-        return pl.pallas_call(
-            put_out,
-            out_shape=out,
-            in_specs=[pl.BlockSpec(memory_space=pltpu.VMEM)] * len(out),
-            out_specs=[pl.BlockSpec(memory_space=pl.ANY)] * len(out),
-            scratch_shapes=[dma((len(out), 2))],
-            compiler_params=pltpu.CompilerParams(vmem_limit_bytes=2**20),
-        )(*(pltpu.with_memory_space_constraint(one, pltpu.VMEM) for one in new))
+        blocks = new[:3]
+        state, token = plain(put_state, new[3:], new[3:], (6, 2))
+        whole, _ = gathered(blocks, weights, token, 1)
+        return (*whole, *state)
 
     all_of, cut = P(None, None, None), P(None, "dp", None)
     return jax.shard_map(

time: 169 us -> 162 us (0.959)
  Pallas kernels: 168 us -> 162 us
    pallas_call x2 -> x4, Pallas kernels: 168 us -> 162 us  [the longest x1 92.4 us: step(): pl.pallas_call(functools.partial(reduce_and_step, n), out_shape=[pltpu.VM...]
where the time goes in v3:
time: 162 us
  Pallas kernels  162 us (100%)
    pallas_call x1, Pallas kernels, step(): pl.pallas_call(functools.partial(reduce_and_step, n), out_shape=[pltpu.VM...  92.4 us
    pallas_call x1, Pallas kernels, gathered(): pl.pallas_call(functools.partial(gather, n, count), out_shape=[pltpu.VMEM...  63.6 us
    pallas_call x2, Pallas kernels, plain(): pl.pallas_call(body, out_shape=[*(jax.ShapeDtypeStruct(one.shape, one.dty...  5.55 us

profile of v3, /device:TPU:22, one launch (start us, length us, event | category | flops | bytes accessed | tf_op | source)
XLA Modules:
  0.0 162.3 jit_solution(8536037426954609128)
XLA Ops:
  0.6 92.4 %shard_map.187 = (bf16[2,64,1280]{2,1,0:T(8,128)(2,1)S(1)}, bf16[2,64,1280]{2,1,0:T(8,128)(2,1)S(1)}, bf16[2,160,512]{2,1,0:T(8,128)(2,1)S(1)}, f32[2,64,1280]{2...) custom-call(bf16[2,512,1280]{2,1,0:T(8,128)(2,1)} %bitcast.3, ...), custom_call_target="tpu_custom_call" | custom-call | tf_op jit(solution)/shard_map/pallas_call | solution.py:339
  93.1 2.0 %shard_map.188 = (f32[2,64,1280]{2,1,0:T(8,128)}, f32[2,64,1280]{2,1,0:T(8,128)}, f32[2,160,512]{2,1,0:T(8,128)}, f32[2,64,1280]{2,1,0:T(8,128)}, f32[2,64,1280]...) custom-call(f32[2,64,1280]{2,1,0:T(8,128)S(1)} %get-tuple-element.34.refs_0_, ...), custom_call_target="tpu_custom_call" | custom-call | tf_op jit(solution)/shard_map/pallas_call | solution.py:315
  95.1 63.6 %shard_map.189 = (bf16[2,512,1280]{2,1,0:T(8,128)(2,1)S(1)}, bf16[2,512,1280]{2,1,0:T(8,128)(2,1)S(1)}, bf16[2,1280,512]{2,1,0:T(8,128)(2,1)S(1)}) custom-call(bf16[2,64,1280]{2,1,0:T(8,128)(2,1)S(1)} %get-tuple-element.31.refs_0_, bf16[2,64,1280]{2,1,0:T(8,128)(2,1)S(1)} %get-tuple-element.32.refs_1_, bf16[2,160,512]{2,1,0:T(8,128)(2,1)S(1)} %get-tuple-element.33.refs_2_, ...), custom_call_target="tpu_custom_call" | custom-call | tf_op jit(solution)/shard_map/pallas_call | solution.py:327
  158.7 3.5 %shard_map.190 = (bf16[2,512,1280]{2,1,0:T(8,128)(2,1)}, bf16[2,512,1280]{2,1,0:T(8,128)(2,1)}, bf16[2,1280,512]{2,1,0:T(8,128)(2,1)}, f32[8,128]{1,0:T(8,128)}) custom-call(bf16[2,64,1280]{2,1,0:T(8,128)(2,1)S(1)} %get-tuple-element.31.refs_0_, bf16[2,64,1280]{2,1,0:T(8,128)(2,1)S(1)} %get-tuple-element.32.refs_1_, ...), custom_call_target="tpu_custom_call" | custom-call | tf_op jit(solution)/shard_map/pallas_call | solution.py:315

commit v4 on v3

--- a/solution.py
+++ b/solution.py
@@ -11,14 +11,26 @@
 F32, BF16 = jnp.float32, jnp.bfloat16
 ROWS, LANES = 16, 256
 
-LATE, HEAD_START_NS = 0, 13000
-
-
-def reduce_and_step(n, *refs):
+LATE, HEAD_START_NS = 0, 12000
+NEAR = 2
+
+
+def pieces(rows, cols, body, carry):
+    def step(i, carry):
+        r = pl.multiple_of(i * ROWS, ROWS)
+        for c in range(0, cols, LANES):
+            carry = body(r, pl.ds(c, LANES), carry)
+        return carry
+
+    return lax.fori_loop(0, rows // ROWS, step, carry)
+
+
+def reduce_and_norm(n, *refs):
     terms, weights, m_in, v_in = (refs[i : i + 3] for i in (0, 3, 6, 9))
-    w_out, m_out, v_out = (refs[i : i + 3] for i in (12, 15, 18))
-    own, arrived, total, w_old, m, v = (refs[i : i + 3] for i in (21, 24, 27, 30, 33, 36))
-    squares, load_sem, state_sem, rs_send, rs_recv, sq_send, sq_recv = refs[39:]
+    total, w_old, m, v = (refs[i : i + 3] for i in (12, 15, 18, 21))
+    factor, *refs = refs[24:]
+    own, arrived = refs[:3], refs[3:6]
+    squares, load_sem, state_sem, rs_send, rs_recv, sq_send, sq_recv = refs[6:]
 
     half = n // 2
     me = lax.axis_index("dp")
@@ -99,15 +111,6 @@
                 need(weight, sign[way] * distance(k))
                 send_sum(way, k, weight).start()
 
-    def pieces(weight, body, carry=None):
-        def step(i, carry):
-            r = pl.multiple_of(i * ROWS, ROWS)
-            for c in range(0, cols[weight], LANES):
-                carry = body(r, pl.ds(c, LANES), carry)
-            return carry
-
-        return lax.fori_loop(0, rows[weight] // ROWS, step, carry)
-
     def add(way, k, weight):
         offset, which = sign[way] * (distance(k) - 1), layer(way, k)
         base = block(weight, offset)
@@ -118,7 +121,7 @@
             arrived[weight][way, k, pl.ds(r, ROWS), c] = (so_far + term).astype(BF16)
             return carry
 
-        pieces(weight, body, 0)
+        pieces(rows[weight], cols[weight], body, 0)
 
     for k in range(sends - 2):
         for weight in range(3):
@@ -143,7 +146,7 @@
             g = g * g
             return sums + (g[:8] + g[8:])
 
-        return pieces(weight, body, sums)
+        return pieces(rows[weight], cols[weight], body, sums)
 
     for weight in range(3):
         need(weight, 0)
@@ -181,33 +184,46 @@
         send_squares(offset).wait_recv()
         everyone += squares[offset, :1]
     everyone = jnp.sum(everyone, axis=1, keepdims=True)
-    factor = jnp.minimum(1.0, 0.5 * lax.rsqrt(everyone / count + 1e-30))
-
-    def adamw(which, weight):
-        def body(r, c, carry):
-            part = (which, pl.ds(r, ROWS), c)
-            g = total[weight][part].astype(F32) * factor
-            w = w_old[weight][part].astype(F32)
-            m_new = 0.9 * m[weight][part] + 0.1 * g
-            v_new = 0.95 * v[weight][part] + 0.05 * g * g
-            m_out[weight][part] = m_new
-            v_out[weight][part] = v_new
-            step = m_new * lax.rsqrt(v_new + 1e-8) + 0.1 * w
-            w_out[weight][part] = (w - 0.02 * step).astype(BF16)
-            return carry
-
-        pieces(weight, body, 0)
-
-    for which in range(2):
-        for weight in range(3):
-            adamw(which, weight)
+    factor[...] = jnp.broadcast_to(jnp.minimum(1.0, 0.5 * lax.rsqrt(everyone / count + 1e-30)), factor.shape)
 
     for offset in far_first:
         send_squares(offset).wait_send()
 
 
-def gather(n, count, *refs):
-    blocks, whole = refs[:count], refs[count + 1 : 2 * count + 1]
+def adamw(*refs):
+    total, w_old, m, v = (refs[i : i + 3] for i in (0, 3, 6, 9))
+    factor = refs[12][:1, :1]
+    w_new, m_out, v_out = (refs[i : i + 3] for i in (13, 16, 19))
+    m_new, v_new = refs[23:26], refs[26:29]
+    sem = refs[29]
+    copies = []
+    for which in range(2):
+        for weight in range(3):
+
+            def body(r, c, carry, which=which, weight=weight):
+                part = (which, pl.ds(r, ROWS), c)
+                g = total[weight][part].astype(F32) * factor
+                w = w_old[weight][part].astype(F32)
+                moment = 0.9 * m[weight][part] + 0.1 * g
+                second = 0.95 * v[weight][part] + 0.05 * g * g
+                m_new[weight][part] = moment
+                v_new[weight][part] = second
+                step = moment * lax.rsqrt(second + 1e-8) + 0.1 * w
+                w_new[weight][part] = (w - 0.02 * step).astype(BF16)
+                return carry
+
+            pieces(m[weight].shape[1], m[weight].shape[2], body, 0)
+            for i, (source, target) in enumerate(((m_new, m_out), (v_new, v_out))):
+                copy = pltpu.make_async_copy(source[weight].at[which], target[weight].at[which], sem.at[i, which, weight])
+                copy.start()
+                copies.append(copy)
+    for copy in copies:
+        copy.wait()
+
+
+def gather(n, first, last, *refs):
+    count = (len(refs) - 3) // 2
+    before, whole = refs[:count], refs[count + 1 : 2 * count + 1]
     sends, recvs = refs[2 * count + 1 :]
     half = n // 2
     me = lax.axis_index("dp")
@@ -222,61 +238,61 @@
     pl.semaphore_wait(barrier, 2)
 
     def copy(way, q, which, weight, behind):
-        rows = blocks[weight].shape[1]
-        place = whole[weight].at[which, pl.ds(pl.multiple_of(at(-sign[way] * behind) * rows, rows), rows)]
+        rows = whole[weight].shape[1] // n
+        part = (which, pl.ds(pl.multiple_of(at(-sign[way] * behind) * rows, rows), rows))
+        if behind == 0:
+            source = before[weight].at[which]
+        else:
+            source = (before if behind == first else whole)[weight].at[part]
         return pltpu.make_async_remote_copy(
-            src_ref=blocks[weight].at[which] if behind == 0 else place,
-            dst_ref=place,
-            send_sem=sends.at[way, q, which, weight],
-            recv_sem=recvs.at[way, q, which, weight],
+            src_ref=source,
+            dst_ref=whole[weight].at[part],
+            send_sem=sends.at[way, q - first, which, weight],
+            recv_sem=recvs.at[way, q - first, which, weight],
             device_id={"dp": at(sign[way])},
             device_id_type=MESH,
         )
 
     def goes(way, q, which):
-        return q < half - 1 or (q == half - 1 and which == way)
-
-    for q in range(half + 1):
-        for which in range(2):
-            for weight in range(count):
-                for way in range(2):
-                    if q and goes(way, q - 1, which):
-                        copy(way, q - 1, which, weight, q).wait_recv()
-                    if goes(way, q, which):
-                        copy(way, q, which, weight, q).start()
-                    if q > 1:
-                        copy(way, q - 2, which, weight, q - 2).wait_send()
-    for which in range(2):
-        for weight in range(count):
-            copy(which, half - 1, which, weight, half - 1).wait_send()
-
-
-def put_state(*refs):
-    arrays = len(refs) // 2 - 1
-    sem = refs[-1]
-    copies = [
-        pltpu.make_async_copy(refs[i].at[layer], refs[arrays + i].at[layer], sem.at[i, layer])
-        for i in range(arrays)
-        for layer in range(2)
-    ]
-    for copy in copies:
-        copy.start()
-    for copy in copies:
-        copy.wait()
-
-
-def put_weights(n, count, *refs):
-    blocks, whole, out = refs[:count], refs[count : 2 * count], refs[2 * count : 3 * count]
-    sem = refs[-1]
+        return q < half - 1 or which == way
+
+    def keep(which, weight):
+        rows, cols = before[weight].shape[1:]
+
+        def body(r, c, carry):
+            whole[weight][which, pl.ds(pl.multiple_of(me * rows + r, ROWS), ROWS), c] = before[weight][which, pl.ds(r, ROWS), c]
+            return carry
+
+        pieces(rows, cols, body, 0)
+
+    each = [(which, weight) for which in range(2) for weight in range(count)]
+    for q in range(first, last + 1):
+        for which, weight in each:
+            for way in range(2):
+                if q > first and goes(way, q - 1, which):
+                    copy(way, q - 1, which, weight, q).wait_recv()
+                if q < last and goes(way, q, which):
+                    copy(way, q, which, weight, q).start()
+                if q > first + 1:
+                    copy(way, q - 2, which, weight, q - 2).wait_send()
+        if q == 0:
+            for which, weight in each:
+                keep(which, weight)
+    for which, weight in each:
+        for way in range(2):
+            if goes(way, last - 1, which):
+                copy(way, last - 1, which, weight, last - 1).wait_send()
+
+
+def put_out(n, offsets, *refs):
+    whole, out, sem = refs[:3], refs[-5:-2], refs[-1]
     me = lax.axis_index("dp")
     copies = []
-    for i in range(count):
-        rows = blocks[i].shape[1]
-        for layer in range(2):
-            for offset in range(n):
-                part = pl.ds(pl.multiple_of(lax.rem(me + offset, n) * rows, rows), rows)
-                source = blocks[i].at[layer] if offset == 0 else whole[i].at[layer, part]
-                copies.append(pltpu.make_async_copy(source, out[i].at[layer, part], sem.at[i, layer, offset]))
+    for i in range(3):
+        rows = whole[i].shape[1] // n
+        for j, offset in enumerate(offsets):
+            part = pl.ds(pl.multiple_of(lax.rem(me + offset, n) * rows, rows), rows)
+            copies.append(pltpu.make_async_copy(whole[i].at[:, part], out[i].at[:, part], sem.at[i, j]))
     for copy in copies:
         copy.start()
     for copy in copies:
@@ -294,8 +310,6 @@
         dma = pltpu.SemaphoreType.DMA
         scratch = [pltpu.VMEM(t.shape, t.dtype) for t in terms]
         scratch += [pltpu.VMEM((2, n - 1, *s[1:]), BF16) for s in shapes]
-        scratch += [pltpu.VMEM(s, BF16) for _ in range(2) for s in shapes]
-        scratch += [pltpu.VMEM(s, F32) for _ in range(2) for s in shapes]
         scratch += [
             pltpu.VMEM((n, 8, 128), F32),
             dma((3, n)),
@@ -310,44 +324,55 @@
         def in_vmem(arrays):
             return [pltpu.with_memory_space_constraint(one, pltpu.VMEM) for one in arrays]
 
-        def plain(body, arrays, out, sems):
-            token = jax.ShapeDtypeStruct((8, 128), F32)
-            *out, token = pl.pallas_call(
-                body,
-                out_shape=[*(jax.ShapeDtypeStruct(one.shape, one.dtype) for one in out), token],
-                in_specs=[vmem] * len(arrays),
-                out_specs=[anywhere] * (len(out) + 1),
-                scratch_shapes=[dma(sems)],
-                compiler_params=pltpu.CompilerParams(vmem_limit_bytes=2**20, has_side_effects=True),
-            )(*in_vmem(arrays))
-            return out, token
-
-        def gathered(blocks, shapes, token, collective_id):
-            count = len(blocks)
-            whole = pl.pallas_call(
-                functools.partial(gather, n, count),
-                out_shape=[pltpu.VMEM(one.shape, one.dtype) for one in shapes],
-                in_specs=[vmem] * count + [anywhere],
-                out_specs=[vmem] * count,
-                scratch_shapes=[dma((2, half, 2, count))] * 2,
+        token = jax.ShapeDtypeStruct((8, 128), F32)
+        limit = pltpu.CompilerParams(vmem_limit_bytes=2**20, has_side_effects=True)
+
+        def gathered(before, first, last, after, collective_id):
+            return pl.pallas_call(
+                functools.partial(gather, n, first, last),
+                out_shape=[pltpu.VMEM(one.shape, one.dtype) for one in weights],
+                in_specs=[vmem] * 3 + [anywhere],
+                out_specs=[vmem] * 3,
+                scratch_shapes=[dma((2, last - first, 2, 3))] * 2,
                 compiler_params=pltpu.CompilerParams(collective_id=collective_id, has_side_effects=True, vmem_limit_bytes=2**20),
-            )(*in_vmem(blocks), token)
-            return plain(functools.partial(put_weights, n, count), (*blocks, *whole), shapes, (count, 2, n))
+            )(*in_vmem(before), after)
+
+        def written(whole, offsets, so_far):
+            *out, after = pl.pallas_call(
+                functools.partial(put_out, n, offsets),
+                out_shape=[*(jax.ShapeDtypeStruct(one.shape, one.dtype) for one in weights), token],
+                in_specs=[vmem] * 3 + [anywhere] * len(so_far),
+                out_specs=[anywhere] * 4,
+                scratch_shapes=[dma((3, len(offsets)))],
+                input_output_aliases={3 + i: i for i in range(len(so_far))},
+                compiler_params=limit,
+            )(*in_vmem(whole), *so_far)
+            return out, after
 
         in_hbm = [pltpu.with_memory_space_constraint(one, pltpu.HBM) for one in (*terms, *weights, *m, *v)]
-        results = [(s, BF16) for s in shapes] + [(s, F32) for s in shapes] * 2
-        new = pl.pallas_call(
-            functools.partial(reduce_and_step, n),
+        results = [(s, BF16) for s in shapes] * 2 + [(s, F32) for s in shapes] * 2 + [((8, 128), F32)]
+        summed = pl.pallas_call(
+            functools.partial(reduce_and_norm, n),
             out_shape=[pltpu.VMEM(*one) for one in results],
             in_specs=[hbm] * len(in_hbm),
             out_specs=[vmem] * len(results),
             scratch_shapes=scratch,
-            compiler_params=pltpu.CompilerParams(collective_id=0, has_side_effects=True, vmem_limit_bytes=28 * 2**20),
+            compiler_params=pltpu.CompilerParams(collective_id=0, has_side_effects=True, vmem_limit_bytes=20 * 2**20),
         )(*in_hbm)
-        blocks = new[:3]
-        state, token = plain(put_state, new[3:], new[3:], (6, 2))
-        whole, _ = gathered(blocks, weights, token, 1)
-        return (*whole, *state)
+        *new, after = pl.pallas_call(
+            adamw,
+            out_shape=[pltpu.VMEM(s, BF16) for s in shapes] + [jax.ShapeDtypeStruct(s, F32) for s in shapes] * 2 + [token],
+            in_specs=[vmem] * len(summed),
+            out_specs=[vmem] * 3 + [anywhere] * 7,
+            scratch_shapes=[pltpu.VMEM(s, F32) for s in shapes] * 2 + [dma((2, 2, 3))],
+            compiler_params=pltpu.CompilerParams(vmem_limit_bytes=6 * 2**20, has_side_effects=True),
+        )(*in_vmem(summed))
+        blocks, state = new[:3], new[3:]
+        near = gathered(blocks, 0, NEAR, after, 1)
+        out, after = written(near, [offset % n for offset in range(-NEAR, NEAR + 1)], ())
+        far = gathered(near, NEAR, half, after, 2)
+        out, _ = written(far, range(NEAR + 1, n - NEAR), out)
+        return (*out, *state)
 
     all_of, cut = P(None, None, None), P(None, "dp", None)
     return jax.shard_map(

time: 162 us -> 160 us (0.988)
  Pallas kernels: 162 us -> 159 us
    pallas_call x4 -> x6, Pallas kernels: 162 us -> 159 us  [the longest x1 90.8 us: step(): pl.pallas_call(functools.partial(reduce_and_norm, n), out_shape=[pltpu.VM...]
where the time goes in v4:
time: 160 us
  Pallas kernels  159 us (99%)
    pallas_call x1, Pallas kernels, step(): pl.pallas_call(functools.partial(reduce_and_norm, n), out_shape=[pltpu.VM...  90.8 us
    pallas_call x2, Pallas kernels, gathered(): pl.pallas_call(functools.partial(gather, n, first, last), out_shape=[pltp...  61.8 us
    pallas_call x2, Pallas kernels, written(): pl.pallas_call(functools.partial(put_out, n, offsets), out_shape=[*(jax.S...  4.05 us

profile of v4, /device:TPU:22, one launch (start us, length us, event | category | flops | bytes accessed | tf_op | source)
XLA Modules:
  0.0 160.0 jit_solution(17786575838566831241)
XLA Ops:
  0.6 90.8 %shard_map.187 = (bf16[2,64,1280]{2,1,0:T(8,128)(2,1)S(1)}, bf16[2,64,1280]{2,1,0:T(8,128)(2,1)S(1)}, bf16[2,160,512]{2,1,0:T(8,128)(2,1)S(1)}, bf16[2,64,1280]{...) custom-call(bf16[2,512,1280]{2,1,0:T(8,128)(2,1)} %bitcast.3, ...), custom_call_target="tpu_custom_call" | custom-call | tf_op jit(solution)/shard_map/pallas_call | solution.py:354
  91.5 2.6 %shard_map.188 = (bf16[2,64,1280]{2,1,0:T(8,128)(2,1)S(1)}, bf16[2,64,1280]{2,1,0:T(8,128)(2,1)S(1)}, bf16[2,160,512]{2,1,0:T(8,128)(2,1)S(1)}, f32[2,64,1280]{2...) custom-call(bf16[2,64,1280]{2,1,0:T(8,128)(2,1)S(1)} %get-tuple-elem, ...), custom_call_target="tpu_custom_call" | custom-call | tf_op jit(solution)/shard_map/pallas_call | solution.py:362
  94.1 40.6 %shard_map.189 = (bf16[2,512,1280]{2,1,0:T(8,128)(2,1)S(1)}, bf16[2,512,1280]{2,1,0:T(8,128)(2,1)S(1)}, bf16[2,1280,512]{2,1,0:T(8,128)(2,1)S(1)}) custom-call(bf16[2,64,1280]{2,1,0:T(8,128)(2,1)S(1)} %get-tuple-element.58.refs_0_, bf16[2,64,1280]{2,1,0:T(8,128)(2,1)S(1)} %get-tuple-element.59.refs_1_, bf16[2,160,512]{2,1,0:T(8,128)(2,1)S(1)} %get-tuple-element.60.refs_2_, ...), custom_call_target="tpu_custom_call" | custom-call | tf_op jit(solution)/shard_map/pallas_call | solution.py:331
  134.7 2.4 %shard_map.190 = (bf16[2,512,1280]{2,1,0:T(8,128)(2,1)}, bf16[2,512,1280]{2,1,0:T(8,128)(2,1)}, bf16[2,1280,512]{2,1,0:T(8,128)(2,1)}, f32[8,128]{1,0:T(8,128)S(1)}) custom-call(bf16[2,512,1280]{2,1,0:T(8,128)(2,1)S(1)} %get-tuple-element.62.refs_0_, bf16[2,512,1280]{2,1,0:T(8,128)(2,1)S(1)} %get-tuple-element.63.refs_1_, ...), custom_call_target="tpu_custom_call" | custom-call | tf_op jit(solution)/shard_map/pallas_call | solution.py:341
  137.1 21.2 %shard_map.191 = (bf16[2,512,1280]{2,1,0:T(8,128)(2,1)S(1)}, bf16[2,512,1280]{2,1,0:T(8,128)(2,1)S(1)}, bf16[2,1280,512]{2,1,0:T(8,128)(2,1)S(1)}) custom-call(bf16[2,512,1280]{2,1,0:T(8,128)(2,1)S(1)} %get-tuple-element.62.refs_0_, bf16[2,512,1280]{2,1,0:T(8,128)(2,1)S(1)} %get-tuple-element.63.refs_1_, ...), custom_call_target="tpu_custom_call" | custom-call | tf_op jit(solution)/shard_map/pallas_call | solution.py:331
  158.3 1.7 %shard_map.192 = (bf16[2,512,1280]{2,1,0:T(8,128)(2,1)}, bf16[2,512,1280]{2,1,0:T(8,128)(2,1)}, bf16[2,1280,512]{2,1,0:T(8,128)(2,1)}, f32[8,128]{1,0:T(8,128)}) custom-call(bf16[2,512,1280]{2,1,0:T(8,128)(2,1)S(1)} %get-tuple-element.66.refs_0_, ...), custom_call_target="tpu_custom_call", output_to_operand_aliasing={{0}: (3, {}), {1}: (4, {}), {2}: (5, {})} | custom-call | tf_op jit(solution)/shard_map/pallas_call | solution.py:341

commit v5 on v4

--- a/solution.py
+++ b/solution.py
@@ -11,7 +11,7 @@
 F32, BF16 = jnp.float32, jnp.bfloat16
 ROWS, LANES = 16, 256
 
-LATE, HEAD_START_NS = 0, 12000
+LATE, HEAD_START_NS = 0, 11500
 NEAR = 2
 
 
@@ -129,7 +129,9 @@
                 need(weight, sign[way] * (distance(k) - 1))
                 send_sum(way, k, weight).wait_recv()
                 add(way, k, weight)
+            for way in range(2):
                 send_sum(way, k + 2, weight).start()
+            for way in range(2):
                 send_sum(way, k, weight).wait_send()
 
     def finish(which, weight, sums):
@@ -171,11 +173,12 @@
         )
 
     far_first = sorted(range(1, n), key=lambda offset: -min(offset, n - offset))
+    for weight in range(3):
+        for which in range(3):
+            state(which, weight).wait()
     for offset in far_first:
         send_squares(offset).start()
     for weight in range(3):
-        for which in range(3):
-            state(which, weight).wait()
         for way in range(2):
             for k in range(sends - 2, sends):
                 send_sum(way, k, weight).wait_send()

time: 160 us -> 160 us (level)
  no operation moved by 1% of the time
where the time goes in v5:
time: 160 us
  Pallas kernels  159 us (99%)
    pallas_call x1, Pallas kernels, step(): pl.pallas_call(functools.partial(reduce_and_norm, n), out_shape=[pltpu.VM...  90.3 us
    pallas_call x2, Pallas kernels, gathered(): pl.pallas_call(functools.partial(gather, n, first, last), out_shape=[pltp...  62.3 us
    pallas_call x2, Pallas kernels, written(): pl.pallas_call(functools.partial(put_out, n, offsets), out_shape=[*(jax.S...  4.05 us

profile of v5, /device:TPU:22, one launch (start us, length us, event | category | flops | bytes accessed | tf_op | source)
XLA Modules:
  0.0 160.0 jit_solution(8602806365625806253)
XLA Ops:
  0.6 90.3 %shard_map.187 = (bf16[2,64,1280]{2,1,0:T(8,128)(2,1)S(1)}, bf16[2,64,1280]{2,1,0:T(8,128)(2,1)S(1)}, bf16[2,160,512]{2,1,0:T(8,128)(2,1)S(1)}, bf16[2,64,1280]{...) custom-call(bf16[2,512,1280]{2,1,0:T(8,128)(2,1)} %bitcast.3, ...), custom_call_target="tpu_custom_call" | custom-call | tf_op jit(solution)/shard_map/pallas_call | solution.py:357
  91.0 2.6 %shard_map.188 = (bf16[2,64,1280]{2,1,0:T(8,128)(2,1)S(1)}, bf16[2,64,1280]{2,1,0:T(8,128)(2,1)S(1)}, bf16[2,160,512]{2,1,0:T(8,128)(2,1)S(1)}, f32[2,64,1280]{2...) custom-call(bf16[2,64,1280]{2,1,0:T(8,128)(2,1)S(1)} %get-tuple-elem, ...), custom_call_target="tpu_custom_call" | custom-call | tf_op jit(solution)/shard_map/pallas_call | solution.py:365
  93.6 40.6 %shard_map.189 = (bf16[2,512,1280]{2,1,0:T(8,128)(2,1)S(1)}, bf16[2,512,1280]{2,1,0:T(8,128)(2,1)S(1)}, bf16[2,1280,512]{2,1,0:T(8,128)(2,1)S(1)}) custom-call(bf16[2,64,1280]{2,1,0:T(8,128)(2,1)S(1)} %get-tuple-element.58.refs_0_, bf16[2,64,1280]{2,1,0:T(8,128)(2,1)S(1)} %get-tuple-element.59.refs_1_, bf16[2,160,512]{2,1,0:T(8,128)(2,1)S(1)} %get-tuple-element.60.refs_2_, ...), custom_call_target="tpu_custom_call" | custom-call | tf_op jit(solution)/shard_map/pallas_call | solution.py:334
  134.2 2.4 %shard_map.190 = (bf16[2,512,1280]{2,1,0:T(8,128)(2,1)}, bf16[2,512,1280]{2,1,0:T(8,128)(2,1)}, bf16[2,1280,512]{2,1,0:T(8,128)(2,1)}, f32[8,128]{1,0:T(8,128)S(1)}) custom-call(bf16[2,512,1280]{2,1,0:T(8,128)(2,1)S(1)} %get-tuple-element.62.refs_0_, bf16[2,512,1280]{2,1,0:T(8,128)(2,1)S(1)} %get-tuple-element.63.refs_1_, ...), custom_call_target="tpu_custom_call" | custom-call | tf_op jit(solution)/shard_map/pallas_call | solution.py:344
  136.6 21.7 %shard_map.191 = (bf16[2,512,1280]{2,1,0:T(8,128)(2,1)S(1)}, bf16[2,512,1280]{2,1,0:T(8,128)(2,1)S(1)}, bf16[2,1280,512]{2,1,0:T(8,128)(2,1)S(1)}) custom-call(bf16[2,512,1280]{2,1,0:T(8,128)(2,1)S(1)} %get-tuple-element.62.refs_0_, bf16[2,512,1280]{2,1,0:T(8,128)(2,1)S(1)} %get-tuple-element.63.refs_1_, ...), custom_call_target="tpu_custom_call" | custom-call | tf_op jit(solution)/shard_map/pallas_call | solution.py:334
  158.3 1.7 %shard_map.192 = (bf16[2,512,1280]{2,1,0:T(8,128)(2,1)}, bf16[2,512,1280]{2,1,0:T(8,128)(2,1)}, bf16[2,1280,512]{2,1,0:T(8,128)(2,1)}, f32[8,128]{1,0:T(8,128)}) custom-call(bf16[2,512,1280]{2,1,0:T(8,128)(2,1)S(1)} %get-tuple-element.66.refs_0_, ...), custom_call_target="tpu_custom_call", output_to_operand_aliasing={{0}: (3, {}), {1}: (4, {}), {2}: (5, {})} | custom-call | tf_op jit(solution)/shard_map/pallas_call | solution.py:344

commit v6 on v5

--- a/solution.py
+++ b/solution.py
@@ -270,8 +270,9 @@
 
     each = [(which, weight) for which in range(2) for weight in range(count)]
     for q in range(first, last + 1):
-        for which, weight in each:
-            for way in range(2):
+        for nth, weight in each:
+            for way in range(2):
+                which = (nth + way) % 2
                 if q > first and goes(way, q - 1, which):
                     copy(way, q - 1, which, weight, q).wait_recv()
                 if q < last and goes(way, q, which):

time: 160 us -> 160 us (level)
  no operation moved by 1% of the time
where the time goes in v6:
time: 160 us
  Pallas kernels  159 us (99%)
    pallas_call x1, Pallas kernels, step(): pl.pallas_call(functools.partial(reduce_and_norm, n), out_shape=[pltpu.VM...  90.3 us
    pallas_call x2, Pallas kernels, gathered(): pl.pallas_call(functools.partial(gather, n, first, last), out_shape=[pltp...  62.3 us
    pallas_call x2, Pallas kernels, written(): pl.pallas_call(functools.partial(put_out, n, offsets), out_shape=[*(jax.S...  4.05 us

profile of v6, /device:TPU:22, one launch (start us, length us, event | category | flops | bytes accessed | tf_op | source)
XLA Modules:
  0.0 160.0 jit_solution(15257059592430952498)
XLA Ops:
  0.6 90.3 %shard_map.187 = (bf16[2,64,1280]{2,1,0:T(8,128)(2,1)S(1)}, bf16[2,64,1280]{2,1,0:T(8,128)(2,1)S(1)}, bf16[2,160,512]{2,1,0:T(8,128)(2,1)S(1)}, bf16[2,64,1280]{...) custom-call(bf16[2,512,1280]{2,1,0:T(8,128)(2,1)} %bitcast.3, ...), custom_call_target="tpu_custom_call" | custom-call | tf_op jit(solution)/shard_map/pallas_call | solution.py:358
  91.0 2.6 %shard_map.188 = (bf16[2,64,1280]{2,1,0:T(8,128)(2,1)S(1)}, bf16[2,64,1280]{2,1,0:T(8,128)(2,1)S(1)}, bf16[2,160,512]{2,1,0:T(8,128)(2,1)S(1)}, f32[2,64,1280]{2...) custom-call(bf16[2,64,1280]{2,1,0:T(8,128)(2,1)S(1)} %get-tuple-elem, ...), custom_call_target="tpu_custom_call" | custom-call | tf_op jit(solution)/shard_map/pallas_call | solution.py:366
  93.6 40.6 %shard_map.189 = (bf16[2,512,1280]{2,1,0:T(8,128)(2,1)S(1)}, bf16[2,512,1280]{2,1,0:T(8,128)(2,1)S(1)}, bf16[2,1280,512]{2,1,0:T(8,128)(2,1)S(1)}) custom-call(bf16[2,64,1280]{2,1,0:T(8,128)(2,1)S(1)} %get-tuple-element.58.refs_0_, bf16[2,64,1280]{2,1,0:T(8,128)(2,1)S(1)} %get-tuple-element.59.refs_1_, bf16[2,160,512]{2,1,0:T(8,128)(2,1)S(1)} %get-tuple-element.60.refs_2_, ...), custom_call_target="tpu_custom_call" | custom-call | tf_op jit(solution)/shard_map/pallas_call | solution.py:335
  134.2 2.4 %shard_map.190 = (bf16[2,512,1280]{2,1,0:T(8,128)(2,1)}, bf16[2,512,1280]{2,1,0:T(8,128)(2,1)}, bf16[2,1280,512]{2,1,0:T(8,128)(2,1)}, f32[8,128]{1,0:T(8,128)S(1)}) custom-call(bf16[2,512,1280]{2,1,0:T(8,128)(2,1)S(1)} %get-tuple-element.62.refs_0_, bf16[2,512,1280]{2,1,0:T(8,128)(2,1)S(1)} %get-tuple-element.63.refs_1_, ...), custom_call_target="tpu_custom_call" | custom-call | tf_op jit(solution)/shard_map/pallas_call | solution.py:345
  136.6 21.7 %shard_map.191 = (bf16[2,512,1280]{2,1,0:T(8,128)(2,1)S(1)}, bf16[2,512,1280]{2,1,0:T(8,128)(2,1)S(1)}, bf16[2,1280,512]{2,1,0:T(8,128)(2,1)S(1)}) custom-call(bf16[2,512,1280]{2,1,0:T(8,128)(2,1)S(1)} %get-tuple-element.62.refs_0_, bf16[2,512,1280]{2,1,0:T(8,128)(2,1)S(1)} %get-tuple-element.63.refs_1_, ...), custom_call_target="tpu_custom_call" | custom-call | tf_op jit(solution)/shard_map/pallas_call | solution.py:335
  158.3 1.7 %shard_map.192 = (bf16[2,512,1280]{2,1,0:T(8,128)(2,1)}, bf16[2,512,1280]{2,1,0:T(8,128)(2,1)}, bf16[2,1280,512]{2,1,0:T(8,128)(2,1)}, f32[8,128]{1,0:T(8,128)}) custom-call(bf16[2,512,1280]{2,1,0:T(8,128)(2,1)S(1)} %get-tuple-element.66.refs_0_, ...), custom_call_target="tpu_custom_call", output_to_operand_aliasing={{0}: (3, {}), {1}: (4, {}), {2}: (5, {})} | custom-call | tf_op jit(solution)/shard_map/pallas_call | solution.py:345
